TPU v7x, 32 devices: a whole 2x2x4 slice. The times are simulated.
32 devices in a mesh: member: 4 (over y, x), space: 8 (over z, core).
Axes of the slice: x: 2, y: 2, z: 4, core: 2. Of those that a mesh axis runs over, the one named last changes fastest.
Arguments:
- ensemble_prediction: bfloat16 [4, 300, 128, 128], P('member', None, 'space'), may hold values from -6 to 6
- observed_analysis: bfloat16 [300, 128, 128], P(None, 'space'), may hold values from -6 to 6
- validity_flags: int32 [2, 128, 128], P(None, 'space'), may hold values from 0 to 1, as said below
Outputs:
- point_score: float32 [300, 128, 128], P(None, 'space')
- channel_loss: float32 [300], replicated
Inputs may be any that keep to these rules, and one draw needn't show every extreme that they name: `validity_flags`: 0 or 1 for each point and group; every point of latitude row 11 is valid in both groups.
All inputs are finite; a program needn't handle non-finite values.
Results may differ from a plain program's by a relative error of at most 0.0003.
Values may be sent and summed in bfloat16 or wider, within the bound.
A program may use at most 64 MiB of HBM per device.

v0:
```python
import jax
import jax.numpy as jnp
from jax import lax
from jax.sharding import PartitionSpec as P

VARIABLE_NUMBER = 300
ATMOS = 180
TILE_SITES = 128
LON = 720
ROWS = 360


def per_channel(values):
    is_ocean = jnp.arange(VARIABLE_NUMBER, dtype=jnp.int32) >= ATMOS
    return jnp.where(is_ocean, values[1], values[0])


def shards(ensemble_prediction, observed_analysis, validity_flags):
    blocks_here = observed_analysis.shape[1]
    realization_entries = lax.axis_size("member")
    lat_rows = min(ROWS, blocks_here * lax.axis_size("space") * TILE_SITES // LON)
    first_point = lax.axis_index("space") * (blocks_here * TILE_SITES)
    position = first_point + jnp.arange(blocks_here * TILE_SITES, dtype=jnp.int32).reshape(
        blocks_here, TILE_SITES
    )
    inside = (position < lat_rows * LON).astype(jnp.float32)
    lat_row = (position // LON).astype(jnp.float32)
    cosine = jnp.cos(jnp.pi * ((lat_row + 0.5) / lat_rows - 0.5))
    valid = inside[None] * (validity_flags > 0).astype(jnp.float32)
    weight = cosine[None] * valid
    local_area = jnp.sum(weight, axis=(1, 2))
    local_count = jnp.sum(valid, axis=(1, 2))
    is_ocean = jnp.arange(VARIABLE_NUMBER, dtype=jnp.int32) >= ATMOS
    weight_chan = jnp.where(is_ocean[:, None, None], weight[1][None], weight[0][None])
    coeff = (1.0 - 0.05 / realization_entries) / (
        2.0 * realization_entries * (realization_entries - 1)
    )
    gathered = lax.all_to_all(
        ensemble_prediction, "member", split_axis=2, concat_axis=0, tiled=True
    )
    share = blocks_here // realization_entries
    first_block = lax.axis_index("member") * share
    target_part = lax.dynamic_slice_in_dim(observed_analysis, first_block, share, 1).astype(
        jnp.float32
    )
    accuracy_component = jnp.zeros(target_part.shape, jnp.float32)
    dispersion_component = jnp.zeros(target_part.shape, jnp.float32)
    for leading_realization in range(realization_entries):
        lead = gathered[leading_realization].astype(jnp.float32)
        accuracy_component = accuracy_component + jnp.abs(lead - target_part)
        for trailing_realization in range(leading_realization + 1, realization_entries):
            dispersion_component = dispersion_component + jnp.abs(
                lead - gathered[trailing_realization].astype(jnp.float32)
            )
    partial_crps = accuracy_component / realization_entries - coeff * (2.0 * dispersion_component)
    crps = lax.all_gather(partial_crps, "member", axis=1, tiled=True)
    area_sum, count = lax.psum((local_area, local_count), "space")
    scale_chan = per_channel(count / area_sum)
    point_score = crps * weight_chan * scale_chan[:, None, None]
    score_sums = lax.psum(jnp.sum(point_score, axis=(1, 2)), "space")
    channel_loss = score_sums / per_channel(count)
    return (point_score, channel_loss)


def solution(mesh):
    in_specs = (P("member", None, "space", None), P(None, "space", None), P(None, "space", None))
    out_specs = (P(None, "space", None), P())
    return jax.shard_map(shards, mesh=mesh, in_specs=in_specs, out_specs=out_specs, check_vma=False)
```

profile of v0, /device:TPU:0, one launch (start us, length us, event | category | flops | bytes accessed | tf_op | source)
XLA Modules:
  0.0 100.8 jit_solution(2808371847547564155)
XLA Ops:
  7.2 0.0 copy-start
  7.2 2.7 %copy.11 = bf16[1,300,16,128]{3,1,0,2:T(8,128)(2,1)} copy(bf16[1,300,16,128]{3,2,1,0:T(8,128)(2,1)} %param.3) | data formatting | bytes 2457600 | tf_op args[0]
  9.9 0.0 copy-start.1
  9.9 5.3 %all-to-all-start = ((bf16[1,300,16,128]{3,1,0,2:T(8,128)(2,1)}), bf16[1,300,16,128]{3,1,0,2:T(8,128)(2,1)S(1)}, u32[]{:S(2)}, u32[]{:S(2)}) async-start(bf16[1,300,16,128]{3,1,0,2:T(8,128)(2,1)} %copy.11), calls=%async_computation | async-start | bytes 2490368 | tf_op jit(solution)/shard_map/all_to_all | solution.py:38
  15.2 0.0 all-gather.2.cloned.1.call-start
  15.2 0.0 copy-done
  15.2 0.2 constant_dynamic-slice_fusion
  15.4 15.6 %all-to-all-done = bf16[1,300,16,128]{3,1,0,2:T(8,128)(2,1)S(1)} async-done(((bf16[1,300,16,128]{3,1,0,2:T(8,128)(2,1)}), bf16[1,300,16,128]{3,1,0,2:T(8,128)(2,1)S(1)}, u32[]{:S(2)}, u32[]{:S(2)}) %all-to-all-start) | async-done | bytes 1228832 | tf_op jit(solution)/shard_map/all_to_all | solution.py:38
  31.0 1.6 %fusion.5 = f32[300,4,128]{2,0,1:T(8,128)} fusion(bf16[4,1,300,4,128]{4,2,3,0,1:T(8,128)(2,1)S(1)} %bitcast.33, bf16[4,1,300,4,128]{4,2,3,1,0:T(8,128)(2,1)S(1)} %bitcast.34, bf16[300,4,128]{2,1,0:T(4,128)(2,1)S(1)} %constant_dynamic-slice_fusion), kind=kLoop, calls=%fused_computation.16 | loop fusion | flops 5529600 | bytes 2150400 | tf_op jit(solution)/shard_map/sub | solution.py:55
  32.5 0.0 all-gather.2.cloned.1.call-update
  32.6 0.1 fusion.26
  32.7 0.0 copy-done.1
  32.7 0.1 fusion.31
  32.8 0.1 select_reduce_fusion
  32.9 15.9 %all-reduce = (f32[2]{0:T(128)S(1)}, f32[2]{0:T(128)S(1)}) all-reduce(f32[2]{0:T(128)S(1)} %select_reduce_fusion, f32[2]{0:T(128)S(1)} %get-tuple-element.10), channel_id=1, replica_groups=mesh['member'=4,'space'=8] {'space'}, use_global_device_ids=true, to_apply=%region_1.2 | all-reduce | flops 4 | bytes 32 | tf_op jit(solution)/shard_map/psum | solution.py:57
  48.8 0.6 fusion.33
  49.4 1.3 %broadcast_select_fusion = f32[300]{0:T(512)S(1)} fusion(f32[]{:T(128)} %bitcast.16, f32[]{:T(128)} %bitcast.15), kind=kLoop, calls=%fused_computation.56 | loop fusion | flops 600 | bytes 1208 | tf_op jit(solution)/shard_map/jit(_where)/select_n | solution.py:15
  50.7 0.6 fusion.32
  51.3 20.2 %all-gather.2.cloned.1.call-done = f32[300,16,128]{2,0,1:T(8,128)} async-done(((f32[300,4,128]{2,0,1:T(8,128)}), f32[300,16,128]{2,0,1:T(8,128)}) %all-gather.2.cloned.1.call-update) | async-done | bytes 2457616 | tf_op jit(solution)/shard_map/all_gather | solution.py:56
  71.5 2.2 %fusion.30 = (f32[300]{0:T(512)S(1)}, f32[300,16,128]{2,0,1:T(8,128)S(1)}) fusion(f32[300]{0:T(512)S(1)} %broadcast_select_fusion, f32[300,16,128]{2,0,1:T(8,128)} %all-gather.2.cloned.1.call-done, f32[16,128]{1,0:T(8,128)S(1)} %get-tuple-element.14, f32[16,128]{1,0:T(8,128)S(1)} %get-tuple-element.13, pred[300]{0:T(512)(128)(4,1)S(1)} %iota_compare_fusion), kind=kLoop, calls=%fused_computation.58 | loop fusion | flops 2457300 | bytes 4934284 | tf_op jit(solution)/shard_map/reduce_sum | solution.py:60
  73.7 2.2 %copy.16 = f32[300,16,128]{2,1,0:T(8,128)} copy(f32[300,16,128]{2,0,1:T(8,128)S(1)} %get-tuple-element.9) | data formatting | bytes 4915200
  75.9 16.2 %psum.23 = f32[300]{0:T(512)S(1)} all-reduce(f32[300]{0:T(512)S(1)} %get-tuple-element.8), channel_id=1, replica_groups=mesh['member'=4,'space'=8] {'space'}, use_global_device_ids=true, to_apply=%region_5.6 | all-reduce | flops 300 | bytes 2400 | tf_op jit(solution)/shard_map/psum | solution.py:60
  92.1 1.9 %select_divide_fusion = f32[300]{0:T(512)} fusion(f32[300]{0:T(512)S(1)} %psum.23, f32[]{:T(128)} %bitcast.18, f32[]{:T(128)} %bitcast.17), kind=kLoop, calls=%fused_computation.54 | loop fusion | flops 900 | bytes 2408 | tf_op jit(solution)/shard_map/div | solution.py:61
  (4 shorter events, 0.0 us)
Async XLA Ops:
  7.2 8.1 %copy-start = (bf16[300,16,128]{2,1,0:T(8,128)(2,1)S(1)}, bf16[300,16,128]{2,1,0:T(8,128)(2,1)}, u32[]{:S(2)}) copy-start(bf16[300,16,128]{2,1,0:T(8,128)(2,1)} %param.4) | copy-start | bytes 3686404
  9.9 22.7 %copy-start.1 = (s32[2,16,128]{2,1,0:T(8,128)S(1)}, s32[2,16,128]{2,1,0:T(8,128)}, u32[]{:S(2)}) copy-start(s32[2,16,128]{2,1,0:T(8,128)} %param.5) | copy-start | bytes 49156
  9.9 21.1 %all-to-all-start = ((bf16[1,300,16,128]{3,1,0,2:T(8,128)(2,1)}), bf16[1,300,16,128]{3,1,0,2:T(8,128)(2,1)S(1)}, u32[]{:S(2)}, u32[]{:S(2)}) async-start(bf16[1,300,16,128]{3,1,0,2:T(8,128)(2,1)} %copy.11), calls=%async_computation | async-start | bytes 2490368 | tf_op jit(solution)/shard_map/all_to_all | solution.py:38
  15.2 56.2 %all-gather.2.cloned.1.call-start = ((), (), s32[]{:S(2)}) async-start(), calls=%async_computation.1 | async-start | bytes 3112960 | tf_op jit(solution)/shard_map/all_gather | solution.py:56
Sparse Core Ops, SparseCore 0:
  32.7 38.7 all-gather.1
where the time goes:
time: 101 us
  waiting for transfers between devices  35.8 us (35%)
  blocking collectives  32.1 us (32%)
  between operations  14.1 us (14%)
  other arithmetic  7.25 us (7%)
  local copies, waits for them, and re-layouts  6.33 us (6%)
  starting transfers between devices  5.33 us (5%)
    all_gather x1, waiting for transfers between devices, shards(): crps = lax.all_gather(partial_crps, 'member', axis=1, tiled=True)  20.2 us
    psum x1, blocking collectives, shards(): score_sums = lax.psum(jnp.sum(point_score, axis=(1, 2)), 'space')  16.2 us
    psum x1, blocking collectives, shards(): area_sum, count = lax.psum((local_area, local_count), 'space')  15.9 us
    all_to_all x1, waiting for transfers between devices, shards(): lax.all_to_all(ensemble_prediction, 'member', split_axis=2, concat_axis=0...  15.6 us
    all_to_all x1, starting transfers between devices, shards(): lax.all_to_all(ensemble_prediction, 'member', split_axis=2, concat_axis=0...  5.32 us
    unnamed x6, local copies, waits for them, and re-layouts  4.95 us
    reduce_sum x1, other arithmetic, shards(): score_sums = lax.psum(jnp.sum(point_score, axis=(1, 2)), 'space')  2.23 us
  transfers between devices with their start and end apart: 2, of which 2 were waited for; matrix products, arithmetic and copies ran while one was open for 3% of the time, Pallas kernels for 0%

commit v1 on v0

v1 whole, which is shorter than its diff:
```python
import functools

import jax
import jax.numpy as jnp
from jax import lax
from jax.experimental import pallas as pl
from jax.experimental.pallas import tpu as pltpu
from jax.sharding import PartitionSpec as P

ATMOS = 180
LON = 720
ROWS = 360
MESH = pl.DeviceIdType.MESH

CODES = 1638.0
CENTRE = 16.0
SMALLEST = 2.0**-36
ABSENT = -32768
INV_LN2 = 1.4426950408889634


def encode(value):
    steps = (jnp.log(jnp.maximum(value, SMALLEST)) * INV_LN2 + CENTRE) * CODES
    code = jnp.floor(steps + 0.5).astype(jnp.int32)
    return jnp.where(value < SMALLEST, ABSENT, code).astype(jnp.int16)


def decode(code):
    code = code.astype(jnp.int32)
    value = jnp.exp2(code.astype(jnp.float32) * (1.0 / CODES) - CENTRE)
    return jnp.where(code == ABSENT, 0.0, value)


def pieces(share, parts):
    edges = [share * i // parts for i in range(parts + 1)]
    return [(a, b - a) for a, b in zip(edges[:-1], edges[1:])]


def kernel(
    members, spaces, share, parts,
    ens_ref, obs_ref, flags_ref,
    code_ref, weight_ref, loss_ref,
    own, target, arrived, totals, stats, sums, gathered,
    local_sem, send_a, recv_a, send_b, recv_b, send_c, recv_c,
    send_s, recv_s, send_t, recv_t, send_u, recv_u,
):
    me = lax.axis_index("member")
    here = lax.axis_index("space")
    x_peer = me + 1 - 2 * lax.rem(me, 2)
    y_peer = lax.rem(me + 2, 4)
    diagonal = 3 - me
    peers = (x_peer, y_peer, diagonal)
    cuts = pieces(share, parts)

    def remote(src, dst, send, recv, where):
        return pltpu.make_async_remote_copy(
            src_ref=src, dst_ref=dst, send_sem=send, recv_sem=recv,
            device_id=where, device_id_type=MESH,
        )

    mine = pltpu.make_async_copy(ens_ref.at[0, pl.ds(me * share, share)], own, local_sem.at[0])
    aim = pltpu.make_async_copy(obs_ref.at[pl.ds(me * share, share)], target, local_sem.at[1])
    mine.start()
    aim.start()

    barrier = pltpu.get_barrier_semaphore()
    for peer in peers:
        pl.semaphore_signal(barrier, inc=1, device_id={"member": peer}, device_id_type=MESH)

    def greet(i, carry):
        pl.semaphore_signal(
            barrier, inc=1, device_id={"space": lax.rem(here + i, spaces)}, device_id_type=MESH
        )
        return carry

    lax.fori_loop(1, spaces, greet, 0)
    pl.semaphore_wait(barrier, 3 + spaces - 1)

    def exchange(j, k):
        first, length = cuts[k]
        return remote(
            ens_ref.at[0, pl.ds(peers[j] * share + first, length)],
            arrived.at[j, pl.ds(first, length)],
            send_a.at[j, k], recv_a.at[j, k], {"member": peers[j]},
        )

    for k in range(parts):
        for j in (2, 0, 1):
            exchange(j, k).start()

    blocks, sites = flags_ref.shape[1], flags_ref.shape[2]
    lat_rows = min(ROWS, blocks * spaces * sites // LON)
    position = (
        here * (blocks * sites)
        + lax.broadcasted_iota(jnp.int32, (blocks, sites), 0) * sites
        + lax.broadcasted_iota(jnp.int32, (blocks, sites), 1)
    )
    inside = (position < lat_rows * LON).astype(jnp.float32)
    row = jnp.floor((position.astype(jnp.float32) + 0.5) * (1.0 / LON))
    cosine = jnp.cos(jnp.pi * ((row + 0.5) / lat_rows - 0.5))
    weights = []
    for g in range(2):
        valid = inside * (flags_ref[g] > 0).astype(jnp.float32)
        weight = cosine * valid
        weights.append(weight)
        weight_ref[g] = weight
        for r, part in ((g, weight), (2 + g, valid)):
            stats[here, pl.ds(r, 1)] = jnp.sum(part, axis=0, keepdims=True)

    def along_space(buffer, send, recv, i):
        return remote(
            buffer.at[here], buffer.at[here], send.at[i], recv.at[here],
            {"space": lax.rem(here + i, spaces)},
        )

    def from_space(buffer, send, recv, i):
        peer = lax.rem(here + i, spaces)
        return remote(
            buffer.at[peer], buffer.at[peer], send.at[i], recv.at[peer], {"space": peer}
        )

    def each_space(make, act):
        def step(i, carry):
            act(make(i))
            return carry

        lax.fori_loop(1, spaces, step, 0)

    each_space(functools.partial(along_space, stats, send_s, recv_s), lambda c: c.start())

    coeff = (1.0 - 0.05 / members) / (2.0 * members * (members - 1))
    totals[...] = jnp.zeros_like(totals)
    mine.wait()
    aim.wait()

    def score(j, k):
        first, length = cuts[k]
        at = code_ref.at[pl.ds(me * share + first, length)]
        return remote(at, at, send_b.at[j, k], recv_b.at[j, k], {"member": peers[j]})

    for k in range(parts):
        first, length = cuts[k]
        for j in range(3):
            exchange(j, k).wait_recv()

        def channel(c, carry, first=first):
            at = first + c
            f32 = lambda v: v.astype(jnp.float32)
            values = [f32(own[at])] + [f32(arrived[j, at]) for j in range(3)]
            goal = f32(target[at])
            skill = sum(jnp.abs(v - goal) for v in values)
            spread = sum(
                jnp.abs(values[a] - values[b]) for a in range(4) for b in range(a + 1, 4)
            )
            crps = skill / members - coeff * (2.0 * spread)
            code_ref[me * share + at] = encode(crps)
            ocean = (me * share + at >= ATMOS).astype(jnp.float32)
            weight = weights[0] * (1.0 - ocean) + weights[1] * ocean
            totals[pl.ds(at, 1)] = jnp.sum(crps * weight, axis=0, keepdims=True)
            return carry

        lax.fori_loop(0, length, channel, 0, unroll=True)
        for j in range(2):
            score(j, k).start()

    sums[here] = lax.dot_general(
        jnp.ones((8, totals.shape[1]), jnp.float32), totals[...],
        (((1,), (1,)), ((), ())),
        precision=lax.Precision.HIGHEST, preferred_element_type=jnp.float32,
    )
    each_space(functools.partial(along_space, sums, send_t, recv_t), lambda c: c.start())

    each_space(functools.partial(from_space, stats, send_s, recv_s), lambda c: c.wait_recv())

    def add(buffer):
        return lax.fori_loop(
            1, spaces, lambda i, t: t + buffer[i], buffer[0]
        )

    whole = add(stats)
    area = [jnp.sum(whole[g : g + 1], axis=1, keepdims=True) for g in range(2)]
    count = [jnp.sum(whole[2 + g : 3 + g], axis=1, keepdims=True) for g in range(2)]
    scale = [count[g] / area[g] for g in range(2)]
    for g in range(2):
        weight_ref[g] = weights[g] * scale[g]

    def share_sums(j):
        return remote(
            gathered.at[me], gathered.at[me], send_u.at[j], recv_u.at[me], {"member": peers[j]}
        )

    def send_sums():
        each_space(functools.partial(from_space, sums, send_t, recv_t), lambda c: c.wait_recv())
        gathered[me] = add(sums)
        for j in range(3):
            share_sums(j).start()

    def relayed(k):
        return (0, 1) if k % 2 == 0 else (1, 0)

    def arrival(j, k):
        first, length = cuts[k]
        at = code_ref.at[pl.ds(peers[j] * share + first, length)]
        return remote(at, at, send_b.at[j, k], recv_b.at[j, k], {"member": peers[j]})

    def relay(k):
        source, goal = relayed(k)
        first, length = cuts[k]
        at = code_ref.at[pl.ds(peers[source] * share + first, length)]
        return remote(at, at, send_c.at[k], recv_c.at[k], {"member": peers[goal]})

    for k in range(parts):
        arrival(relayed(k)[0], k).wait_recv()
        relay(k).start()
        if k == parts // 2:
            send_sums()

    for j in range(3):
        remote(
            gathered.at[peers[j]], gathered.at[peers[j]], send_u.at[j], recv_u.at[peers[j]],
            {"member": peers[j]},
        ).wait_recv()
    channel_at = (
        lax.broadcasted_iota(jnp.int32, (members, totals.shape[0]), 0) * share
        + lax.broadcasted_iota(jnp.int32, (members, totals.shape[0]), 1)
    )
    rows = jnp.concatenate([gathered[m, 0:1] for m in range(members)], axis=0)
    loss_ref[...] = jnp.where(
        channel_at >= ATMOS, rows * scale[1] / count[1], rows * scale[0] / count[0]
    )
    for k in range(parts):
        arrival(relayed(k)[1], k).wait_recv()
        first, length = cuts[k]
        at = code_ref.at[pl.ds(diagonal * share + first, length)]
        remote(at, at, send_c.at[k], recv_c.at[k], {"member": diagonal}).wait_recv()
    for k in range(parts):
        for j in range(3):
            exchange(j, k).wait_send()
        for j in range(2):
            score(j, k).wait_send()
        relay(k).wait_send()
    each_space(functools.partial(along_space, stats, send_s, recv_s), lambda c: c.wait_send())
    each_space(functools.partial(along_space, sums, send_t, recv_t), lambda c: c.wait_send())
    for j in range(3):
        share_sums(j).wait_send()


def shards(spaces, parts, ensemble_prediction, observed_analysis, validity_flags):
    members = lax.axis_size("member")
    channels, blocks, sites = observed_analysis.shape
    share = channels // members
    dma = pltpu.SemaphoreType.DMA
    wide = -(-share // 128) * 128
    code, weight, loss = pl.pallas_call(
        functools.partial(kernel, members, spaces, share, parts),
        out_shape=(
            jax.ShapeDtypeStruct((channels, blocks, sites), jnp.int16),
            jax.ShapeDtypeStruct((2, blocks, sites), jnp.float32),
            jax.ShapeDtypeStruct((members, wide), jnp.float32),
        ),
        in_specs=[
            pl.BlockSpec(memory_space=pl.ANY),
            pl.BlockSpec(memory_space=pl.ANY),
            pl.BlockSpec(memory_space=pltpu.VMEM),
        ],
        out_specs=(pl.BlockSpec(memory_space=pltpu.VMEM),) * 3,
        scratch_shapes=[
            pltpu.VMEM((share, blocks, sites), jnp.bfloat16),
            pltpu.VMEM((share, blocks, sites), jnp.bfloat16),
            pltpu.VMEM((3, share, blocks, sites), jnp.bfloat16),
            pltpu.VMEM((wide, sites), jnp.float32),
            pltpu.VMEM((spaces, 8, sites), jnp.float32),
            pltpu.VMEM((spaces, 8, wide), jnp.float32),
            pltpu.VMEM((members, 8, wide), jnp.float32),
            dma((2,)),
            dma((3, parts)), dma((3, parts)),
            dma((2, parts)), dma((2, parts)),
            dma((parts,)), dma((parts,)),
            dma((spaces,)), dma((spaces,)),
            dma((spaces,)), dma((spaces,)),
            dma((3,)), dma((members,)),
        ],
        compiler_params=pltpu.CompilerParams(collective_id=0, has_side_effects=True),
    )(ensemble_prediction, observed_analysis, validity_flags)
    is_ocean = jnp.arange(channels, dtype=jnp.int32) >= ATMOS
    weight_chan = jnp.where(is_ocean[:, None, None], weight[1][None], weight[0][None])
    return decode(code) * weight_chan, loss[:, :share].reshape(channels)


def solution(mesh):
    in_specs = (P("member", None, "space", None), P(None, "space", None), P(None, "space", None))
    out_specs = (P(None, "space", None), P())
    return jax.shard_map(
        functools.partial(shards, mesh.shape["space"], 6),
        mesh=mesh, in_specs=in_specs, out_specs=out_specs, check_vma=False,
    )
```

time: 101 us -> 41.1 us (0.41)
  waiting for transfers between devices: 35.8 us -> 0 us
  Pallas kernels: 0 us -> 34.5 us
  blocking collectives: 32.1 us -> 0 us
  between operations: 14.1 us -> 0.64 us
  starting transfers between devices: 5.33 us -> 0 us
  local copies, waits for them, and re-layouts: 6.33 us -> 2.05 us
  other arithmetic: 7.25 us -> 3.55 us
    pallas_call x0 -> x1, Pallas kernels: none -> 34.5 us  [shards(): pl.pallas_call(functools.partial(kernel, members, spaces, share, parts),...]
    psum x2 -> x0, blocking collectives: 32.1 us -> none  [the longest x1 16.2 us: shards(): score_sums = lax.psum(jnp.sum(point_score, axis=(1, 2)), 'space')]
    all_gather x1 -> x0, waiting for transfers between devices: 20.2 us -> none  [shards(): crps = lax.all_gather(partial_crps, 'member', axis=1, tiled=True)]
    all_to_all x1 -> x0, waiting for transfers between devices: 15.6 us -> none  [shards(): lax.all_to_all(ensemble_prediction, 'member', split_axis=2, concat_axis=0...]
    all_to_all x1 -> x0, starting transfers between devices: 5.32 us -> none  [shards(): lax.all_to_all(ensemble_prediction, 'member', split_axis=2, concat_axis=0...]
    unnamed x6 -> x0, local copies, waits for them, and re-layouts: 4.95 us -> none
    mul x0 -> x1, other arithmetic: none -> 3.55 us  [shards(): return (decode(code) * weight_chan, loss[:, :share].reshape(channels))]
    reduce_sum x3 -> x0, other arithmetic: 2.43 us -> none  [the longest x1 2.23 us: shards(): score_sums = lax.psum(jnp.sum(point_score, axis=(1, 2)), 'space')]
  transfers between devices with their start and end apart: 2 -> 0, of which waited for: 2 -> 0; matrix products, arithmetic and copies ran while one was open for 3% -> 0% of each run, Pallas kernels for 0% -> 0%
where the time goes in v1:
time: 41.1 us; the launch traced here: 40.7 us
  Pallas kernels  34.5 us (84%)
  other arithmetic  3.55 us (9%)
  local copies, waits for them, and re-layouts  2.05 us (5%)
  between operations  0.64 us (2%)
    pallas_call x1, Pallas kernels, shards(): pl.pallas_call(functools.partial(kernel, members, spaces, share, parts),...  34.5 us
    mul x1, other arithmetic, shards(): return (decode(code) * weight_chan, loss[:, :share].reshape(channels))  3.55 us
    reshape x1, local copies, waits for them, and re-layouts, shards(): return (decode(code) * weight_chan, loss[:, :share].reshape(channels))  1.33 us

profile of v1, /device:TPU:0, one launch (start us, length us, event | category | flops | bytes accessed | tf_op | source)
XLA Modules:
  0.0 40.7 jit_solution(17810355627891757844)
XLA Ops:
  0.6 34.5 %shard_map.50 = (s16[300,16,128]{2,1,0:T(8,128)(2,1)}, f32[2,16,128]{2,1,0:T(8,128)}, f32[4,128]{1,0:T(4,128)}) custom-call(bf16[1,300,16,128]{3,2,1,0:T(8,128)(2,1)} %ens_ref.1, bf16[300,16,128]{2,1,0:T(8,128)(2,1)} %obs_ref.1, s32[2,16,128]{2,1,0:T(8,128)} %flags_ref.1), custom_call_target="tpu_custom_call" | custom-call | tf_op jit(solution)/shard_map/pallas_call | solution.py:254
  35.1 1.3 %reshape.11 = f32[300]{0:T(512)} reshape(f32[4,75]{1,0:T(4,128)} %bitcast.5) | data formatting | bytes 2400 | tf_op jit(solution)/shard_map/reshape | solution.py:287
  36.4 0.7 %slice_bitcast_fusion.1 = (f32[16,128]{1,0:T(8,128)S(1)}, f32[16,128]{1,0:T(8,128)S(1)}) fusion(f32[2,16,128]{2,1,0:T(8,128)} %get-tuple-element.6), kind=kLoop, calls=%fused_computation.9 | loop fusion | bytes 32768 | tf_op jit(solution)/shard_map/jit(_where)/broadcast_in_dim | solution.py:286
  37.2 3.5 %fusion.5 = f32[300,16,128]{2,1,0:T(8,128)} fusion(s16[300,16,128]{2,1,0:T(8,128)(2,1)} %get-tuple-element.5, f32[16,128]{1,0:T(8,128)S(1)} %get-tuple-element.9, f32[16,128]{1,0:T(8,128)S(1)} %get-tuple-element.8, pred[300]{0:T(512)(128)(4,1)S(1)} %iota_compare_fusion), kind=kLoop, calls=%fused_computation.7 | loop fusion | flops 5529600 | bytes 3703084 | tf_op jit(solution)/shard_map/mul | solution.py:287
  (1 shorter events, 0.0 us)

commit v2 on v1

--- a/solution.py
+++ b/solution.py
@@ -16,6 +16,7 @@
 CENTRE = 16.0
 SMALLEST = 2.0**-36
 ABSENT = -32768
+PLAN = ((1,),(1,),(1,))
 INV_LN2 = 1.4426950408889634
 
 
@@ -31,16 +32,22 @@
     return jnp.where(code == ABSENT, 0.0, value)
 
 
-def pieces(share, parts):
-    edges = [share * i // parts for i in range(parts + 1)]
-    return [(a, b - a) for a, b in zip(edges[:-1], edges[1:])]
+def pieces(share, plan):
+    flat = [w for group in plan for w in group]
+    edges = [share * sum(flat[:i]) // sum(flat) for i in range(len(flat) + 1)]
+    cuts = [(a, b - a) for a, b in zip(edges[:-1], edges[1:])]
+    groups, at = [], 0
+    for group in plan:
+        groups.append(range(at, at + len(group)))
+        at += len(group)
+    return cuts, groups
 
 
 def kernel(
-    members, spaces, share, parts,
-    ens_ref, obs_ref, flags_ref,
-    code_ref, weight_ref, loss_ref,
-    own, target, arrived, totals, stats, sums, gathered,
+    members, spaces, share, plan,
+    ens_ref, obs_ref, flags_in,
+    score_ref, loss_out,
+    flags_ref, loss_ref, code_ref, own, target, arrived, totals, stats, sums, gathered,
     local_sem, send_a, recv_a, send_b, recv_b, send_c, recv_c,
     send_s, recv_s, send_t, recv_t, send_u, recv_u,
 ):
@@ -50,7 +57,8 @@
     y_peer = lax.rem(me + 2, 4)
     diagonal = 3 - me
     peers = (x_peer, y_peer, diagonal)
-    cuts = pieces(share, parts)
+    cuts, groups = pieces(share, plan)
+    parts = len(cuts)
 
     def remote(src, dst, send, recv, where):
         return pltpu.make_async_remote_copy(
@@ -60,6 +68,9 @@
 
     mine = pltpu.make_async_copy(ens_ref.at[0, pl.ds(me * share, share)], own, local_sem.at[0])
     aim = pltpu.make_async_copy(obs_ref.at[pl.ds(me * share, share)], target, local_sem.at[1])
+    flags = pltpu.make_async_copy(flags_in, flags_ref, local_sem.at[2])
+    loss = pltpu.make_async_copy(loss_ref, loss_out, local_sem.at[3])
+    flags.start()
     mine.start()
     aim.start()
 
@@ -77,14 +88,15 @@
     pl.semaphore_wait(barrier, 3 + spaces - 1)
 
     def exchange(j, k):
-        first, length = cuts[k]
+        first = cuts[groups[k][0]][0]
+        length = sum(cuts[i][1] for i in groups[k])
         return remote(
             ens_ref.at[0, pl.ds(peers[j] * share + first, length)],
             arrived.at[j, pl.ds(first, length)],
             send_a.at[j, k], recv_a.at[j, k], {"member": peers[j]},
         )
 
-    for k in range(parts):
+    for k in range(len(groups)):
         for j in (2, 0, 1):
             exchange(j, k).start()
 
@@ -98,12 +110,12 @@
     inside = (position < lat_rows * LON).astype(jnp.float32)
     row = jnp.floor((position.astype(jnp.float32) + 0.5) * (1.0 / LON))
     cosine = jnp.cos(jnp.pi * ((row + 0.5) / lat_rows - 0.5))
+    flags.wait()
     weights = []
     for g in range(2):
         valid = inside * (flags_ref[g] > 0).astype(jnp.float32)
         weight = cosine * valid
         weights.append(weight)
-        weight_ref[g] = weight
         for r, part in ((g, weight), (2 + g, valid)):
             stats[here, pl.ds(r, 1)] = jnp.sum(part, axis=0, keepdims=True)
 
@@ -140,8 +152,10 @@
 
     for k in range(parts):
         first, length = cuts[k]
-        for j in range(3):
-            exchange(j, k).wait_recv()
+        for i in range(len(groups)):
+            if k == groups[i][0]:
+                for j in range(3):
+                    exchange(j, i).wait_recv()
 
         def channel(c, carry, first=first):
             at = first + c
@@ -156,7 +170,7 @@
             code_ref[me * share + at] = encode(crps)
             ocean = (me * share + at >= ATMOS).astype(jnp.float32)
             weight = weights[0] * (1.0 - ocean) + weights[1] * ocean
-            totals[pl.ds(at, 1)] = jnp.sum(crps * weight, axis=0, keepdims=True)
+            totals[pl.ds(me * share + at, 1)] = jnp.sum(crps * weight, axis=0, keepdims=True)
             return carry
 
         lax.fori_loop(0, length, channel, 0, unroll=True)
@@ -181,8 +195,18 @@
     area = [jnp.sum(whole[g : g + 1], axis=1, keepdims=True) for g in range(2)]
     count = [jnp.sum(whole[2 + g : 3 + g], axis=1, keepdims=True) for g in range(2)]
     scale = [count[g] / area[g] for g in range(2)]
-    for g in range(2):
-        weight_ref[g] = weights[g] * scale[g]
+    scaled = [weights[g] * scale[g] for g in range(2)]
+
+    def show(owner, k):
+        first, length = cuts[k]
+
+        def channel(c, carry):
+            at = owner * share + first + c
+            ocean = (at >= ATMOS).astype(jnp.float32)
+            score_ref[at] = decode(code_ref[at]) * (scaled[0] * (1.0 - ocean) + scaled[1] * ocean)
+            return carry
+
+        lax.fori_loop(0, length, channel, 0, unroll=True)
 
     def share_sums(j):
         return remote(
@@ -210,32 +234,42 @@
         return remote(at, at, send_c.at[k], recv_c.at[k], {"member": peers[goal]})
 
     for k in range(parts):
-        arrival(relayed(k)[0], k).wait_recv()
+        show(me, k)
+
+    def finish(k):
+        first, length = cuts[k]
+        at = code_ref.at[pl.ds(diagonal * share + first, length)]
+        remote(at, at, send_c.at[k], recv_c.at[k], {"member": diagonal}).wait_recv()
+        show(diagonal, k)
+
+    for k in range(parts):
+        source, goal = relayed(k)
+        arrival(source, k).wait_recv()
         relay(k).start()
+        show(peers[source], k)
         if k == parts // 2:
             send_sums()
+        arrival(goal, k).wait_recv()
+        show(peers[goal], k)
+        if k >= 2:
+            finish(k - 2)
 
     for j in range(3):
         remote(
             gathered.at[peers[j]], gathered.at[peers[j]], send_u.at[j], recv_u.at[peers[j]],
             {"member": peers[j]},
         ).wait_recv()
-    channel_at = (
-        lax.broadcasted_iota(jnp.int32, (members, totals.shape[0]), 0) * share
-        + lax.broadcasted_iota(jnp.int32, (members, totals.shape[0]), 1)
-    )
-    rows = jnp.concatenate([gathered[m, 0:1] for m in range(members)], axis=0)
-    loss_ref[...] = jnp.where(
-        channel_at >= ATMOS, rows * scale[1] / count[1], rows * scale[0] / count[0]
-    )
-    for k in range(parts):
-        arrival(relayed(k)[1], k).wait_recv()
-        first, length = cuts[k]
-        at = code_ref.at[pl.ds(diagonal * share + first, length)]
-        remote(at, at, send_c.at[k], recv_c.at[k], {"member": diagonal}).wait_recv()
-    for k in range(parts):
+    line = sum(gathered[m] for m in range(members))[0:1]
+    channel_at = lax.broadcasted_iota(jnp.int32, line.shape, 1)
+    line = jnp.where(channel_at >= ATMOS, line * scale[1] / count[1], line * scale[0] / count[0])
+    loss_ref[...] = line.reshape(line.shape[1])[: loss_ref.shape[0]]
+    loss.start()
+    for k in range(max(parts - 2, 0), parts):
+        finish(k)
+    for k in range(len(groups)):
         for j in range(3):
             exchange(j, k).wait_send()
+    for k in range(parts):
         for j in range(2):
             score(j, k).wait_send()
         relay(k).wait_send()
@@ -243,28 +277,31 @@
     each_space(functools.partial(along_space, sums, send_t, recv_t), lambda c: c.wait_send())
     for j in range(3):
         share_sums(j).wait_send()
-
-
-def shards(spaces, parts, ensemble_prediction, observed_analysis, validity_flags):
+    loss.wait()
+
+
+def shards(spaces, plan, ensemble_prediction, observed_analysis, validity_flags):
     members = lax.axis_size("member")
     channels, blocks, sites = observed_analysis.shape
     share = channels // members
     dma = pltpu.SemaphoreType.DMA
-    wide = -(-share // 128) * 128
-    code, weight, loss = pl.pallas_call(
-        functools.partial(kernel, members, spaces, share, parts),
+    exchanges, parts = len(plan), sum(len(group) for group in plan)
+    wide = -(-channels // 128) * 128
+    return pl.pallas_call(
+        functools.partial(kernel, members, spaces, share, plan),
         out_shape=(
-            jax.ShapeDtypeStruct((channels, blocks, sites), jnp.int16),
-            jax.ShapeDtypeStruct((2, blocks, sites), jnp.float32),
-            jax.ShapeDtypeStruct((members, wide), jnp.float32),
+            pltpu.VMEM((channels, blocks, sites), jnp.float32),
+            pltpu.HBM((channels,), jnp.float32),
         ),
-        in_specs=[
-            pl.BlockSpec(memory_space=pl.ANY),
-            pl.BlockSpec(memory_space=pl.ANY),
+        in_specs=[pl.BlockSpec(memory_space=pltpu.HBM)] * 3,
+        out_specs=(
             pl.BlockSpec(memory_space=pltpu.VMEM),
-        ],
-        out_specs=(pl.BlockSpec(memory_space=pltpu.VMEM),) * 3,
+            pl.BlockSpec(memory_space=pltpu.HBM),
+        ),
         scratch_shapes=[
+            pltpu.VMEM(validity_flags.shape, jnp.int32),
+            pltpu.VMEM((channels,), jnp.float32),
+            pltpu.VMEM((channels, blocks, sites), jnp.int16),
             pltpu.VMEM((share, blocks, sites), jnp.bfloat16),
             pltpu.VMEM((share, blocks, sites), jnp.bfloat16),
             pltpu.VMEM((3, share, blocks, sites), jnp.bfloat16),
@@ -272,25 +309,27 @@
             pltpu.VMEM((spaces, 8, sites), jnp.float32),
             pltpu.VMEM((spaces, 8, wide), jnp.float32),
             pltpu.VMEM((members, 8, wide), jnp.float32),
-            dma((2,)),
-            dma((3, parts)), dma((3, parts)),
+            dma((4,)),
+            dma((3, exchanges)), dma((3, exchanges)),
             dma((2, parts)), dma((2, parts)),
             dma((parts,)), dma((parts,)),
             dma((spaces,)), dma((spaces,)),
             dma((spaces,)), dma((spaces,)),
             dma((3,)), dma((members,)),
         ],
-        compiler_params=pltpu.CompilerParams(collective_id=0, has_side_effects=True),
-    )(ensemble_prediction, observed_analysis, validity_flags)
-    is_ocean = jnp.arange(channels, dtype=jnp.int32) >= ATMOS
-    weight_chan = jnp.where(is_ocean[:, None, None], weight[1][None], weight[0][None])
-    return decode(code) * weight_chan, loss[:, :share].reshape(channels)
+        compiler_params=pltpu.CompilerParams(
+            collective_id=0, has_side_effects=True, vmem_limit_bytes=16 * 2**20
+        ),
+    )(*(
+        pltpu.with_memory_space_constraint(v, pltpu.HBM)
+        for v in (ensemble_prediction, observed_analysis, validity_flags)
+    ))
 
 
 def solution(mesh):
     in_specs = (P("member", None, "space", None), P(None, "space", None), P(None, "space", None))
     out_specs = (P(None, "space", None), P())
     return jax.shard_map(
-        functools.partial(shards, mesh.shape["space"], 6),
+        functools.partial(shards, mesh.shape["space"], PLAN),
         mesh=mesh, in_specs=in_specs, out_specs=out_specs, check_vma=False,
     )

time: 41.1 us -> 36.3 us (0.88)
  other arithmetic: 3.55 us -> 0 us
  Pallas kernels: 34.5 us -> 33.4 us
    mul x1 -> x0, other arithmetic: 3.55 us -> none  [shards(): return (decode(code) * weight_chan, loss[:, :share].reshape(channels))]
    unnamed x0 -> x4, local copies, waits for them, and re-layouts: none -> 2.02 us
    reshape x1 -> x0, local copies, waits for them, and re-layouts: 1.33 us -> none  [shards(): return (decode(code) * weight_chan, loss[:, :share].reshape(channels))]
    pallas_call x1, Pallas kernels: 34.5 us -> 33.4 us  [shards(): pl.pallas_call(functools.partial(kernel, members, spaces, share, plan), o...]
    broadcast_in_dim x1 -> x0, local copies, waits for them, and re-layouts: 0.72 us -> none  [shards(): jnp.where(is_ocean[:, None, None], weight[1][None], weight[0][None])]
where the time goes in v2:
time: 36.3 us; the launch traced here: 36.1 us
  Pallas kernels  33.4 us (92%)
  local copies, waits for them, and re-layouts  2.02 us (6%)
  between operations  0.65 us (2%)
    pallas_call x1, Pallas kernels, shards(): pl.pallas_call(functools.partial(kernel, members, spaces, share, plan), o...  33.4 us
    unnamed x4, local copies, waits for them, and re-layouts  2.02 us

profile of v2, /device:TPU:0, one launch (start us, length us, event | category | flops | bytes accessed | tf_op | source)
XLA Modules:
  0.0 36.1 jit_solution(4309818122227250045)
XLA Ops:
  0.6 33.4 %shard_map.50 = (f32[300,16,128]{2,1,0:T(8,128)S(1)}, f32[300]{0:T(512)}) custom-call(bf16[1,300,16,128]{3,2,1,0:T(8,128)(2,1)} %ens_ref.1, bf16[300,16,128]{2,1,0:T(8,128)(2,1)} %obs_ref.1, s32[2,16,128]{2,1,0:T(8,128)} %flags_in.1), custom_call_target="tpu_custom_call" | custom-call | tf_op jit(solution)/shard_map/pallas_call | solution.py:290
  34.1 0.0 copy-start
  34.1 1.4 %copy.7 = f32[300,16,128]{2,1,0:T(8,128)} copy(f32[300,16,128]{2,1,0:T(8,128)S(1)} %get-tuple-element.2) | data formatting | bytes 4915200
  35.5 0.0 copy-done
  35.5 0.6 %copy.8 = f32[300]{0:T(512)} copy(f32[300]{0:T(512)S(1)} %copy-done) | data formatting | bytes 2400
Async XLA Ops:
  34.1 1.5 %copy-start = (f32[300]{0:T(512)S(1)}, f32[300]{0:T(512)}, u32[]{:S(2)}) copy-start(f32[300]{0:T(512)} %get-tuple-element.7) | copy-start | bytes 3604
